TPU v7x, 32 devices: a whole 2x2x4 slice. The times are simulated.
32 devices in a mesh: rows: 8 (over z, y), feat: 4 (over x, core).
Axes of the slice: x: 2, y: 2, z: 4, core: 2. Of those that a mesh axis runs over, the one named last changes fastest.
Arguments:
- bin_index: int32 [16384, 512], P('rows', 'feat'), may hold values from 0 to 255
- leaf_ids: int32 [16384], P('rows'), may hold values from 0 to 15
- gradients: bfloat16 [16384], P('rows'), may hold values from -3 to 3
- hessians: bfloat16 [16384], P('rows'), may hold values from 0.049804688 to 0.25
Outputs:
- split_gains: float32 [4, 128, 16, 256], P('feat', 'rows')
- best_gain: float32 [16], replicated
All inputs are finite; a program needn't handle non-finite values.
Results may differ from a plain program's by a relative error of at most 0.0003.
Values may be sent and summed in bfloat16 or wider, within the bound.
A program may use at most 64 MiB of HBM per device.

v0:
```python
import functools

import jax
import jax.numpy as jnp
from jax import lax
from jax.experimental import pallas as pl
from jax.experimental.pallas import tpu as pltpu
from jax.sharding import PartitionSpec as P

BINS = 256
LEAVES = 16
LANES = 128
HALF = BINS // 2
MESH = pl.DeviceIdType.MESH

reg_lambda = 1.0


def kernel(n, n_feat, group, bins_hbm, leaf_hbm, grad_hbm, hess_hbm, gain_ref, best_ref,
           leaf_ref, grad_ref, hess_ref, small_sems, raw, bins_src, meta_src, columns, metas, weights, sums, top, landing,
           raw_sems, bin_send, bin_recv, meta_send, meta_recv, own_sems, top_send, top_recv):
    me, me_feat = lax.axis_index("rows"), lax.axis_index("feat")
    everyone = n * n_feat
    me_all = me * n_feat + me_feat
    own, rows = bins_src.shape[1], bins_src.shape[2]
    tiles = rows // LANES
    pieces = raw_sems.shape[0]
    piece_rows = rows // pieces

    def fetch(piece):
        span = pl.ds(piece * piece_rows, piece_rows)
        return pltpu.make_async_copy(bins_hbm.at[span], raw.at[span], raw_sems.at[piece])

    small = [pltpu.make_async_copy(source, target, small_sems.at[place]) for place, (source, target) in enumerate(
        ((leaf_hbm, leaf_ref), (grad_hbm, grad_ref), (hess_hbm, hess_ref)))]
    for piece in range(pieces):
        fetch(piece).start()
    for copy in small:
        copy.start()

    def device_after(step):
        other = lax.rem(me_all + step, everyone)
        return {"rows": other // n_feat, "feat": lax.rem(other, n_feat)}

    barrier = pltpu.get_barrier_semaphore()

    def greet(step, carry):
        pl.semaphore_signal(barrier, inc=1, device_id=device_after(step), device_id_type=MESH)
        return carry

    lax.fori_loop(1, everyone, greet, 0)

    for copy in small:
        copy.wait()
    meta_src[:tiles] = leaf_ref[...].astype(jnp.float32).astype(jnp.bfloat16)
    meta_src[tiles:2 * tiles] = grad_ref[...]
    meta_src[2 * tiles:] = hess_ref[...]
    for piece in range(pieces):
        fetch(piece).wait()
        for tile in range(piece * piece_rows // LANES, (piece + 1) * piece_rows // LANES):
            lanes = slice(tile * LANES, (tile + 1) * LANES)
            turned = raw[lanes].astype(jnp.float32).T.astype(jnp.bfloat16)
            bins_src[:, :, lanes] = turned.reshape(n, own, LANES)

    own_bins = pltpu.make_async_copy(bins_src.at[me], columns.at[me], own_sems.at[0])
    own_meta = pltpu.make_async_copy(meta_src, metas.at[me], own_sems.at[1])
    own_bins.start()
    own_meta.start()
    pl.semaphore_wait(barrier, everyone - 1)

    def partner(step):
        other, bit = 0, 1
        while bit < n:
            other += lax.rem(me // bit + step // bit, 2) * bit
            bit *= 2
        return other

    def exchange(step, landed):
        other = partner(step)
        place = other if landed else me
        copies = []
        for source, target, send_sems, recv_sems in (
                (meta_src, metas, meta_send, meta_recv), (bins_src.at[other], columns, bin_send, bin_recv)):
            copies.append(pltpu.make_async_remote_copy(
                src_ref=source, dst_ref=target.at[place], send_sem=send_sems.at[step],
                recv_sem=recv_sems.at[step], device_id={"rows": other}, device_id_type=MESH))
        return copies

    def start_sends(step, carry):
        for copy in exchange(step, False):
            copy.start()
        return carry

    lax.fori_loop(1, n, start_sends, 0)
    sums[...] = jnp.zeros_like(sums)
    own_bins.wait()
    own_meta.wait()

    def one_shard(step, carry):
        origin = partner(step)

        @pl.when(step > 0)
        def arrived():
            for copy in exchange(step, True):
                copy.wait_recv()

        table = metas[origin].astype(jnp.float32)
        leaf_of = lax.broadcasted_iota(jnp.int32, (LEAVES, LANES), 0).astype(jnp.float32)
        for tile in range(tiles):
            member = jnp.broadcast_to(table[tile:tile + 1], (LEAVES, LANES)) == leaf_of
            for part in (0, 1):
                first = (1 + part) * tiles + tile
                value = jnp.broadcast_to(table[first:first + 1], (LEAVES, LANES))
                weights[part * LEAVES:(part + 1) * LEAVES, tile * LANES:(tile + 1) * LANES] = (
                    jnp.where(member, value, 0.0).astype(jnp.bfloat16))

        block = columns[origin]
        level = lax.broadcasted_iota(jnp.int32, (HALF, rows), 0).astype(jnp.bfloat16)
        one, zero = jnp.ones((), jnp.bfloat16), jnp.zeros((), jnp.bfloat16)
        table_rows = weights[...]
        for first in range(0, own, group):
            left_side, right_side = [], []
            for feature in range(first, first + group):
                bins = block[feature:feature + 1]
                upper = bins >= HALF
                low = jnp.where(upper, bins - HALF, bins)
                upper_wide = jnp.broadcast_to(bins, (2 * LEAVES, rows)) >= HALF
                left_side.append(jnp.where(upper_wide, zero, table_rows))
                left_side.append(jnp.where(upper_wide, table_rows, zero))
                right_side.append(jnp.where(jnp.broadcast_to(low, (HALF, rows)) <= level, one, zero).astype(jnp.float8_e4m3fn))
            product = lax.dot_general(
                jnp.concatenate(left_side, axis=0), jnp.concatenate(right_side, axis=0),
                (((1,), (1,)), ((), ())), preferred_element_type=jnp.float32)
            for place in range(group):
                sums[first + place] += product[place * 4 * LEAVES:(place + 1) * 4 * LEAVES, place * HALF:(place + 1) * HALF]
        return carry

    lax.fori_loop(0, n, one_shard, 0)

    def gains(feature, largest):
        part = sums[feature]
        grad_low, hess_low = part[:LEAVES], part[LEAVES:2 * LEAVES]
        grad_high = part[2 * LEAVES:3 * LEAVES] + grad_low[:, HALF - 1:]
        hess_high = part[3 * LEAVES:] + hess_low[:, HALF - 1:]
        total_grad, total_hess = grad_high[:, HALF - 1:], hess_high[:, HALF - 1:]
        whole = total_grad * total_grad / (total_hess + reg_lambda)
        for place, left_grad, left_hess in ((0, grad_low, hess_low), (1, grad_high, hess_high)):
            right_grad, right_hess = total_grad - left_grad, total_hess - left_hess
            gain = 0.5 * (left_grad * left_grad / (left_hess + reg_lambda)
                          + right_grad * right_grad / (right_hess + reg_lambda) - whole)
            gain_ref[feature, :, place * HALF:(place + 1) * HALF] = gain
            largest = jnp.maximum(largest, gain)
        return largest

    largest = lax.fori_loop(0, own, gains, jnp.full((LEAVES, HALF), -jnp.inf, jnp.float32), unroll=True)
    largest = jnp.broadcast_to(jnp.max(largest, axis=1, keepdims=True), (LEAVES, LANES))
    on_lane = (lax.broadcasted_iota(jnp.int32, (LEAVES, LANES), 0) == lax.broadcasted_iota(jnp.int32, (LEAVES, LANES), 1))
    top[...] = jnp.max(jnp.where(on_lane, largest, -jnp.inf), axis=0, keepdims=True)

    def report(step):
        return pltpu.make_async_remote_copy(
            src_ref=top, dst_ref=landing.at[step], send_sem=top_send.at[step],
            recv_sem=top_recv.at[step], device_id=device_after(step), device_id_type=MESH)

    def start_report(step, carry):
        report(step).start()
        return carry

    def collect(step, best):
        report(step).wait_recv()
        return jnp.maximum(best, landing[step])

    def finish(step, carry):
        report(step).wait_send()
        return carry

    def finish_sends(step, carry):
        for copy in exchange(step, False):
            copy.wait_send()
        return carry

    lax.fori_loop(1, everyone, start_report, 0)
    lax.fori_loop(1, n, finish_sends, 0)
    best = lax.fori_loop(1, everyone, collect, top[...])
    lax.fori_loop(1, everyone, finish, 0)
    best_ref[...] = best[:, :LEAVES]


def body(bin_index, leaf_ids, gradients, hessians):
    n, n_feat = lax.axis_size("rows"), lax.axis_size("feat")
    rows, local_features = bin_index.shape
    own = local_features // n
    group = 2 if own % 2 == 0 else 1
    tiles = rows // LANES
    pieces = 4
    everyone = n * n_feat
    vmem = pl.BlockSpec(memory_space=pltpu.VMEM)
    dma = pltpu.SemaphoreType.DMA
    gain, best = pl.pallas_call(
        functools.partial(kernel, n, n_feat, group),
        out_shape=(pltpu.VMEM((own, LEAVES, BINS), jnp.float32),
                   pltpu.VMEM((1, LEAVES), jnp.float32)),
        in_specs=[pl.BlockSpec(memory_space=pl.ANY)] * 4,
        out_specs=(vmem, vmem),
        scratch_shapes=[
            pltpu.VMEM((tiles, LANES), jnp.int32),
            pltpu.VMEM((tiles, LANES), jnp.bfloat16),
            pltpu.VMEM((tiles, LANES), jnp.bfloat16),
            dma((3,)),
            pltpu.VMEM((rows, local_features), jnp.int32),
            pltpu.VMEM((n, own, rows), jnp.bfloat16),
            pltpu.VMEM((3 * tiles, LANES), jnp.bfloat16),
            pltpu.VMEM((n, own, rows), jnp.bfloat16),
            pltpu.VMEM((n, 3 * tiles, LANES), jnp.bfloat16),
            pltpu.VMEM((2 * LEAVES, rows), jnp.bfloat16),
            pltpu.VMEM((own, 4 * LEAVES, HALF), jnp.float32),
            pltpu.VMEM((1, LANES), jnp.float32),
            pltpu.VMEM((everyone, 1, LANES), jnp.float32),
            dma((pieces,)), dma((n,)), dma((n,)), dma((n,)), dma((n,)), dma((2,)),
            dma((everyone,)), dma((everyone,)),
        ],
        compiler_params=pltpu.CompilerParams(
            collective_id=0, has_side_effects=True, vmem_limit_bytes=60 * 1024 * 1024),
    )(bin_index, leaf_ids.reshape(tiles, LANES), gradients.reshape(tiles, LANES), hessians.reshape(tiles, LANES))
    return gain[None], best.reshape(LEAVES)


def solution(mesh):
    placed = (P("rows", "feat"), P("rows"), P("rows"), P("rows"))
    return jax.shard_map(
        body,
        mesh=mesh,
        in_specs=placed,
        out_specs=(P("feat", "rows", None, None), P()),
        check_vma=False,
    )
```

profile of v0, /device:TPU:0, one launch (start us, length us, event | category | flops | bytes accessed | tf_op | source)
XLA Modules:
  0.0 31.1 jit_solution(7761218286315700508)
XLA Ops:
  0.6 29.3 %shard_map.59 = (f32[16,16,256]{2,1,0:T(8,128)S(1)}, f32[1,16]{1,0:T(1,128)S(1)}) custom-call(s32[2048,128]{1,0:T(8,128)} %bins_hbm.1, s32[16,128]{1,0:T(8,128)} %bitcast.7, bf16[16,128]{1,0:T(8,128)(2,1)} %bitcast.8, bf16[16,128]{1,0:T(8,128)(2,1)} %bitcast.9), custom_call_target="tpu_custom_call" | custom-call | tf_op jit(solution)/shard_map/pallas_call | solution.py:199
  29.9 0.7 %copy.8 = f32[1,16,16,256]{3,2,1,0:T(8,128)} copy(f32[1,16,16,256]{3,2,1,0:T(8,128)S(1)} %bitcast.5) | data formatting | bytes 524288
  30.6 0.5 %copy.9 = f32[16]{0:T(128)} copy(f32[16]{0:T(128)S(1)} %bitcast.6) | data formatting | bytes 128
where the time goes:
time: 31.3 us; the launch traced here: 31.1 us
  Pallas kernels  29.3 us (94%)
  local copies, waits for them, and re-layouts  1.22 us (4%)
  between operations  0.64 us (2%)
    pallas_call x1, Pallas kernels, body(): pl.pallas_call(functools.partial(kernel, n, n_feat, group), out_shape=(pl...  29.3 us
    unnamed x2, local copies, waits for them, and re-layouts  1.22 us

commit v1 on v0

--- a/solution.py
+++ b/solution.py
@@ -18,12 +18,15 @@
 
 def kernel(n, n_feat, group, bins_hbm, leaf_hbm, grad_hbm, hess_hbm, gain_ref, best_ref,
            leaf_ref, grad_ref, hess_ref, small_sems, raw, bins_src, meta_src, columns, metas, weights, sums, top, landing,
-           raw_sems, bin_send, bin_recv, meta_send, meta_recv, own_sems, top_send, top_recv):
+           raw_sems, bin_send, bin_recv, meta_send, meta_recv, swap_send, swap_recv, own_sems, top_send, top_recv):
     me, me_feat = lax.axis_index("rows"), lax.axis_index("feat")
     everyone = n * n_feat
     me_all = me * n_feat + me_feat
     own, rows = bins_src.shape[1], bins_src.shape[2]
     tiles = rows // LANES
+    share = tiles // n_feat
+    half = n // 2
+    across = (1 - me // half) * half
     pieces = raw_sems.shape[0]
     piece_rows = rows // pieces
 
@@ -33,28 +36,42 @@
 
     small = [pltpu.make_async_copy(source, target, small_sems.at[place]) for place, (source, target) in enumerate(
         ((leaf_hbm, leaf_ref), (grad_hbm, grad_ref), (hess_hbm, hess_ref)))]
+    for copy in small:
+        copy.start()
     for piece in range(pieces):
         fetch(piece).start()
-    for copy in small:
-        copy.start()
+
+    def partner(step):
+        other, bit = 0, 1
+        while bit < n:
+            other += lax.rem(me // bit + step // bit, 2) * bit
+            bit *= 2
+        return other
 
     def device_after(step):
-        other = lax.rem(me_all + step, everyone)
-        return {"rows": other // n_feat, "feat": lax.rem(other, n_feat)}
+        return {"rows": partner(step // n_feat), "feat": lax.rem(me_feat + lax.rem(step, n_feat), n_feat)}
 
     barrier = pltpu.get_barrier_semaphore()
 
-    def greet(step, carry):
-        pl.semaphore_signal(barrier, inc=1, device_id=device_after(step), device_id_type=MESH)
-        return carry
-
-    lax.fori_loop(1, everyone, greet, 0)
+    def each(first, last, act):
+        def run(step, carry):
+            act(step)
+            return carry
+        lax.fori_loop(first, last, run, 0, unroll=everyone <= 64)
+
+    def greet(device):
+        pl.semaphore_signal(barrier, inc=1, device_id=device, device_id_type=MESH)
+
+    each(1, n, lambda step: greet({"rows": partner(n - step)}))
+    each(1, n_feat, lambda step: greet(device_after(step)))
 
     for copy in small:
         copy.wait()
-    meta_src[:tiles] = leaf_ref[...].astype(jnp.float32).astype(jnp.bfloat16)
-    meta_src[tiles:2 * tiles] = grad_ref[...]
-    meta_src[2 * tiles:] = hess_ref[...]
+    leaf, grad, hess = (ref[...].astype(jnp.float32) for ref in (leaf_ref, grad_ref, hess_ref))
+    spare = jnp.zeros((meta_src.shape[1] - 3 * share, LANES), jnp.float32)
+    for part in range(n_feat):
+        span = slice(part * share, (part + 1) * share)
+        meta_src[part] = jnp.concatenate([leaf[span], grad[span], hess[span], spare], axis=0).astype(jnp.bfloat16)
     for piece in range(pieces):
         fetch(piece).wait()
         for tile in range(piece * piece_rows // LANES, (piece + 1) * piece_rows // LANES):
@@ -63,54 +80,72 @@
             bins_src[:, :, lanes] = turned.reshape(n, own, LANES)
 
     own_bins = pltpu.make_async_copy(bins_src.at[me], columns.at[me], own_sems.at[0])
-    own_meta = pltpu.make_async_copy(meta_src, metas.at[me], own_sems.at[1])
+    own_meta = pltpu.make_async_copy(meta_src, metas.at[:, me], own_sems.at[1])
     own_bins.start()
     own_meta.start()
-    pl.semaphore_wait(barrier, everyone - 1)
-
-    def partner(step):
-        other, bit = 0, 1
-        while bit < n:
-            other += lax.rem(me // bit + step // bit, 2) * bit
-            bit *= 2
-        return other
-
-    def exchange(step, landed):
+    pl.semaphore_wait(barrier, n - 1 + n_feat - 1)
+
+    def bin_copy(step, landed):
         other = partner(step)
-        place = other if landed else me
-        copies = []
-        for source, target, send_sems, recv_sems in (
-                (meta_src, metas, meta_send, meta_recv), (bins_src.at[other], columns, bin_send, bin_recv)):
-            copies.append(pltpu.make_async_remote_copy(
-                src_ref=source, dst_ref=target.at[place], send_sem=send_sems.at[step],
-                recv_sem=recv_sems.at[step], device_id={"rows": other}, device_id_type=MESH))
-        return copies
-
-    def start_sends(step, carry):
-        for copy in exchange(step, False):
-            copy.start()
-        return carry
-
-    lax.fori_loop(1, n, start_sends, 0)
+        return pltpu.make_async_remote_copy(
+            src_ref=bins_src.at[other], dst_ref=columns.at[other if landed else me], send_sem=bin_send.at[step],
+            recv_sem=bin_recv.at[step], device_id={"rows": other}, device_id_type=MESH)
+
+    def near_meta(step, landed):
+        other = partner(step)
+        return pltpu.make_async_remote_copy(
+            src_ref=meta_src, dst_ref=metas.at[:, other if landed else me], send_sem=meta_send.at[step],
+            recv_sem=meta_recv.at[step], device_id={"rows": other}, device_id_type=MESH)
+
+    def far_meta(step, landed):
+        other = partner(step)
+        return pltpu.make_async_remote_copy(
+            src_ref=meta_src.at[me_feat], dst_ref=metas.at[me_feat, other if landed else me], send_sem=meta_send.at[step],
+            recv_sem=meta_recv.at[step], device_id={"rows": other}, device_id_type=MESH)
+
+    def swap_meta(step, landed):
+        held = lax.rem(me_feat + n_feat - step, n_feat) if landed else me_feat
+        far = metas.at[held, pl.ds(across, half)]
+        return pltpu.make_async_remote_copy(
+            src_ref=far, dst_ref=far, send_sem=swap_send.at[step], recv_sem=swap_recv.at[step],
+            device_id={"feat": lax.rem(me_feat + step, n_feat)}, device_id_type=MESH)
+
+    each(half, n, lambda step: far_meta(step, False).start())
+    each(1, half, lambda step: near_meta(step, False).start())
+    each(1, n, lambda step: bin_copy(step, False).start())
     sums[...] = jnp.zeros_like(sums)
+    landing[0] = jnp.full((1, LANES), -jnp.inf, jnp.float32)
     own_bins.wait()
     own_meta.wait()
 
     def one_shard(step, carry):
         origin = partner(step)
 
+        @pl.when(step == min(2, half - 1))
+        def swap():
+            each(half, n, lambda far: far_meta(far, True).wait_recv())
+            each(1, n_feat, lambda other: swap_meta(other, False).start())
+
+        @pl.when(jnp.logical_and(step > 0, step < half))
+        def near_arrived():
+            near_meta(step, True).wait_recv()
+
+        @pl.when(step == half)
+        def swapped():
+            each(1, n_feat, lambda other: swap_meta(other, True).wait_recv())
+
         @pl.when(step > 0)
         def arrived():
-            for copy in exchange(step, True):
-                copy.wait_recv()
-
-        table = metas[origin].astype(jnp.float32)
+            bin_copy(step, True).wait_recv()
+
+        table = metas[:, origin].astype(jnp.float32)
         leaf_of = lax.broadcasted_iota(jnp.int32, (LEAVES, LANES), 0).astype(jnp.float32)
         for tile in range(tiles):
-            member = jnp.broadcast_to(table[tile:tile + 1], (LEAVES, LANES)) == leaf_of
+            piece, row = tile // share, tile % share
+            member = jnp.broadcast_to(table[piece, row:row + 1], (LEAVES, LANES)) == leaf_of
             for part in (0, 1):
-                first = (1 + part) * tiles + tile
-                value = jnp.broadcast_to(table[first:first + 1], (LEAVES, LANES))
+                first = (1 + part) * share + row
+                value = jnp.broadcast_to(table[piece, first:first + 1], (LEAVES, LANES))
                 weights[part * LEAVES:(part + 1) * LEAVES, tile * LANES:(tile + 1) * LANES] = (
                     jnp.where(member, value, 0.0).astype(jnp.bfloat16))
 
@@ -157,32 +192,20 @@
     on_lane = (lax.broadcasted_iota(jnp.int32, (LEAVES, LANES), 0) == lax.broadcasted_iota(jnp.int32, (LEAVES, LANES), 1))
     top[...] = jnp.max(jnp.where(on_lane, largest, -jnp.inf), axis=0, keepdims=True)
 
-    def report(step):
+    def report(place):
+        step = everyone - place
         return pltpu.make_async_remote_copy(
             src_ref=top, dst_ref=landing.at[step], send_sem=top_send.at[step],
             recv_sem=top_recv.at[step], device_id=device_after(step), device_id_type=MESH)
 
-    def start_report(step, carry):
-        report(step).start()
-        return carry
-
-    def collect(step, best):
-        report(step).wait_recv()
-        return jnp.maximum(best, landing[step])
-
-    def finish(step, carry):
-        report(step).wait_send()
-        return carry
-
-    def finish_sends(step, carry):
-        for copy in exchange(step, False):
-            copy.wait_send()
-        return carry
-
-    lax.fori_loop(1, everyone, start_report, 0)
-    lax.fori_loop(1, n, finish_sends, 0)
-    best = lax.fori_loop(1, everyone, collect, top[...])
-    lax.fori_loop(1, everyone, finish, 0)
+    each(1, everyone, lambda place: report(place).start())
+    each(1, n, lambda step: bin_copy(step, False).wait_send())
+    each(1, half, lambda step: near_meta(step, False).wait_send())
+    each(half, n, lambda step: far_meta(step, False).wait_send())
+    each(1, n_feat, lambda step: swap_meta(step, False).wait_send())
+    each(1, everyone, lambda place: report(everyone - place).wait_recv())
+    best = jnp.maximum(top[...], jnp.max(landing[...], axis=0))
+    each(1, everyone, lambda step: report(step).wait_send())
     best_ref[...] = best[:, :LEAVES]
 
 
@@ -194,6 +217,7 @@
     tiles = rows // LANES
     pieces = 4
     everyone = n * n_feat
+    meta_rows = -(-3 * (tiles // n_feat) // 16) * 16
     vmem = pl.BlockSpec(memory_space=pltpu.VMEM)
     dma = pltpu.SemaphoreType.DMA
     gain, best = pl.pallas_call(
@@ -209,14 +233,14 @@
             dma((3,)),
             pltpu.VMEM((rows, local_features), jnp.int32),
             pltpu.VMEM((n, own, rows), jnp.bfloat16),
-            pltpu.VMEM((3 * tiles, LANES), jnp.bfloat16),
+            pltpu.VMEM((n_feat, meta_rows, LANES), jnp.bfloat16),
             pltpu.VMEM((n, own, rows), jnp.bfloat16),
-            pltpu.VMEM((n, 3 * tiles, LANES), jnp.bfloat16),
+            pltpu.VMEM((n_feat, n, meta_rows, LANES), jnp.bfloat16),
             pltpu.VMEM((2 * LEAVES, rows), jnp.bfloat16),
             pltpu.VMEM((own, 4 * LEAVES, HALF), jnp.float32),
             pltpu.VMEM((1, LANES), jnp.float32),
             pltpu.VMEM((everyone, 1, LANES), jnp.float32),
-            dma((pieces,)), dma((n,)), dma((n,)), dma((n,)), dma((n,)), dma((2,)),
+            dma((pieces,)), dma((n,)), dma((n,)), dma((n,)), dma((n,)), dma((n_feat,)), dma((n_feat,)), dma((2,)),
             dma((everyone,)), dma((everyone,)),
         ],
         compiler_params=pltpu.CompilerParams(

time: 31.3 us -> 29 us (0.927)
  Pallas kernels: 29.3 us -> 27 us
    pallas_call x1, Pallas kernels: 29.3 us -> 27 us  [body(): pl.pallas_call(functools.partial(kernel, n, n_feat, group), out_shape=(pl...]
where the time goes in v1:
time: 29 us; the launch traced here: 28.9 us
  Pallas kernels  27 us (93%)
  local copies, waits for them, and re-layouts  1.22 us (4%)
  between operations  0.64 us (2%)
    pallas_call x1, Pallas kernels, body(): pl.pallas_call(functools.partial(kernel, n, n_feat, group), out_shape=(pl...  27 us
    unnamed x2, local copies, waits for them, and re-layouts  1.22 us

profile of v1, /device:TPU:0, one launch (start us, length us, event | category | flops | bytes accessed | tf_op | source)
XLA Modules:
  0.0 28.9 jit_solution(9705627286457207526)
XLA Ops:
  0.6 27.0 %shard_map.59 = (f32[16,16,256]{2,1,0:T(8,128)S(1)}, f32[1,16]{1,0:T(1,128)S(1)}) custom-call(s32[2048,128]{1,0:T(8,128)} %bins_hbm.1, s32[16,128]{1,0:T(8,128)} %bitcast.7, bf16[16,128]{1,0:T(8,128)(2,1)} %bitcast.8, bf16[16,128]{1,0:T(8,128)(2,1)} %bitcast.9), custom_call_target="tpu_custom_call" | custom-call | tf_op jit(solution)/shard_map/pallas_call | solution.py:223
  27.7 0.7 %copy.8 = f32[1,16,16,256]{3,2,1,0:T(8,128)} copy(f32[1,16,16,256]{3,2,1,0:T(8,128)S(1)} %bitcast.5) | data formatting | bytes 524288
  28.4 0.5 %copy.9 = f32[16]{0:T(128)} copy(f32[16]{0:T(128)S(1)} %bitcast.6) | data formatting | bytes 128

commit v2 on v1

--- a/solution.py
+++ b/solution.py
@@ -11,13 +11,14 @@
 LEAVES = 16
 LANES = 128
 HALF = BINS // 2
+DEPTH = 256
 MESH = pl.DeviceIdType.MESH
 
 reg_lambda = 1.0
 
 
-def kernel(n, n_feat, group, bins_hbm, leaf_hbm, grad_hbm, hess_hbm, gain_ref, best_ref,
-           leaf_ref, grad_ref, hess_ref, small_sems, raw, bins_src, meta_src, columns, metas, weights, sums, top, landing,
+def kernel(n, n_feat, bins_hbm, leaf_hbm, grad_hbm, hess_hbm, gain_ref, best_ref,
+           leaf_ref, grad_ref, hess_ref, small_sems, raw, bins_src, meta_src, columns, metas, weights, top, landing,
            raw_sems, bin_send, bin_recv, meta_send, meta_recv, swap_send, swap_recv, own_sems, top_send, top_recv):
     me, me_feat = lax.axis_index("rows"), lax.axis_index("feat")
     everyone = n * n_feat
@@ -113,12 +114,25 @@
     each(half, n, lambda step: far_meta(step, False).start())
     each(1, half, lambda step: near_meta(step, False).start())
     each(1, n, lambda step: bin_copy(step, False).start())
-    sums[...] = jnp.zeros_like(sums)
     landing[0] = jnp.full((1, LANES), -jnp.inf, jnp.float32)
     own_bins.wait()
     own_meta.wait()
 
-    def one_shard(step, carry):
+    pairs = -(-own // 2)
+
+    def compute(*sums):
+        for total in sums:
+            pltpu.matmul_pop(total)
+        lax.fori_loop(0, n, functools.partial(one_shard, sums), 0)
+        largest = jnp.full((LEAVES, HALF), -jnp.inf, jnp.float32)
+        for pair in range(pairs):
+            largest = gains(pair, pltpu.matmul_pop(sums[pair]), largest)
+        largest = jnp.broadcast_to(jnp.max(largest, axis=1, keepdims=True), (LEAVES, LANES))
+        on_lane = (lax.broadcasted_iota(jnp.int32, (LEAVES, LANES), 0)
+                   == lax.broadcasted_iota(jnp.int32, (LEAVES, LANES), 1))
+        top[...] = jnp.max(jnp.where(on_lane, largest, -jnp.inf), axis=0, keepdims=True)
+
+    def one_shard(sums, step, carry):
         origin = partner(step)
 
         @pl.when(step == min(2, half - 1))
@@ -150,47 +164,59 @@
                     jnp.where(member, value, 0.0).astype(jnp.bfloat16))
 
         block = columns[origin]
-        level = lax.broadcasted_iota(jnp.int32, (HALF, rows), 0).astype(jnp.bfloat16)
-        one, zero = jnp.ones((), jnp.bfloat16), jnp.zeros((), jnp.bfloat16)
-        table_rows = weights[...]
-        for first in range(0, own, group):
-            left_side, right_side = [], []
-            for feature in range(first, first + group):
-                bins = block[feature:feature + 1]
-                upper = bins >= HALF
-                low = jnp.where(upper, bins - HALF, bins)
-                upper_wide = jnp.broadcast_to(bins, (2 * LEAVES, rows)) >= HALF
-                left_side.append(jnp.where(upper_wide, zero, table_rows))
-                left_side.append(jnp.where(upper_wide, table_rows, zero))
-                right_side.append(jnp.where(jnp.broadcast_to(low, (HALF, rows)) <= level, one, zero).astype(jnp.float8_e4m3fn))
-            product = lax.dot_general(
-                jnp.concatenate(left_side, axis=0), jnp.concatenate(right_side, axis=0),
-                (((1,), (1,)), ((), ())), preferred_element_type=jnp.float32)
-            for place in range(group):
-                sums[first + place] += product[place * 4 * LEAVES:(place + 1) * 4 * LEAVES, place * HALF:(place + 1) * HALF]
+        low = jnp.where(block >= HALF, block - HALF, block)
+        level = lax.broadcasted_iota(jnp.int32, (HALF, DEPTH), 0).astype(jnp.bfloat16)
+        zero = jnp.zeros((), jnp.bfloat16)
+        hit, miss = (jnp.full((HALF, DEPTH), value, jnp.float8_e4m3fn) for value in (1, 0))
+
+        def step_of(feature, lanes):
+            reached = jnp.broadcast_to(low[feature:feature + 1, lanes], (HALF, DEPTH)) <= level
+            return jnp.where(reached, hit, miss)
+
+        def upper_of(feature, lanes, table_rows):
+            upper = jnp.broadcast_to(block[feature:feature + 1, lanes], (2 * LEAVES, DEPTH)) >= HALF
+            return jnp.where(upper, table_rows, zero)
+
+        for first in range(0, pairs, 2):
+            for chunk in range(rows // DEPTH):
+                lanes = slice(chunk * DEPTH, (chunk + 1) * DEPTH)
+                table_rows = weights[:, lanes]
+                for pair in range(first, min(first + 2, pairs)):
+                    features = (2 * pair, min(2 * pair + 1, own - 1))
+                    steps = jnp.concatenate([step_of(feature, lanes) for feature in features], axis=0)
+                    turned = (chunk + pair) % 3 != 0
+                    pltpu.matmul_push_rhs(
+                        steps.T if turned else steps,
+                        staging_register=chunk % 2, mxu_index=pair % 2, transpose=not turned)
+                    pltpu.matmul_acc_lhs(
+                        sums[pair],
+                        jnp.concatenate([table_rows] + [upper_of(feature, lanes, table_rows) for feature in features], axis=0),
+                        load_staged_rhs=chunk % 2)
         return carry
 
-    lax.fori_loop(0, n, one_shard, 0)
-
-    def gains(feature, largest):
-        part = sums[feature]
-        grad_low, hess_low = part[:LEAVES], part[LEAVES:2 * LEAVES]
-        grad_high = part[2 * LEAVES:3 * LEAVES] + grad_low[:, HALF - 1:]
-        hess_high = part[3 * LEAVES:] + hess_low[:, HALF - 1:]
-        total_grad, total_hess = grad_high[:, HALF - 1:], hess_high[:, HALF - 1:]
-        whole = total_grad * total_grad / (total_hess + reg_lambda)
-        for place, left_grad, left_hess in ((0, grad_low, hess_low), (1, grad_high, hess_high)):
-            right_grad, right_hess = total_grad - left_grad, total_hess - left_hess
-            gain = 0.5 * (left_grad * left_grad / (left_hess + reg_lambda)
-                          + right_grad * right_grad / (right_hess + reg_lambda) - whole)
-            gain_ref[feature, :, place * HALF:(place + 1) * HALF] = gain
-            largest = jnp.maximum(largest, gain)
+    def gains(pair, part, largest):
+        for place in range(2):
+            feature = 2 * pair + place
+            if feature == own:
+                break
+            lanes = slice(place * HALF, (place + 1) * HALF)
+            both = part[:2 * LEAVES, lanes]
+            upper = part[(1 + place) * 2 * LEAVES:(2 + place) * 2 * LEAVES, lanes]
+            lower = both - upper
+            grad_low, hess_low = lower[:LEAVES], lower[LEAVES:]
+            grad_high = upper[:LEAVES] + grad_low[:, HALF - 1:]
+            hess_high = upper[LEAVES:] + hess_low[:, HALF - 1:]
+            total_grad, total_hess = grad_high[:, HALF - 1:], hess_high[:, HALF - 1:]
+            whole = total_grad * total_grad / (total_hess + reg_lambda)
+            for side, left_grad, left_hess in ((0, grad_low, hess_low), (1, grad_high, hess_high)):
+                right_grad, right_hess = total_grad - left_grad, total_hess - left_hess
+                gain = 0.5 * (left_grad * left_grad / (left_hess + reg_lambda)
+                              + right_grad * right_grad / (right_hess + reg_lambda) - whole)
+                gain_ref[feature, :, side * HALF:(side + 1) * HALF] = gain
+                largest = jnp.maximum(largest, gain)
         return largest
 
-    largest = lax.fori_loop(0, own, gains, jnp.full((LEAVES, HALF), -jnp.inf, jnp.float32), unroll=True)
-    largest = jnp.broadcast_to(jnp.max(largest, axis=1, keepdims=True), (LEAVES, LANES))
-    on_lane = (lax.broadcasted_iota(jnp.int32, (LEAVES, LANES), 0) == lax.broadcasted_iota(jnp.int32, (LEAVES, LANES), 1))
-    top[...] = jnp.max(jnp.where(on_lane, largest, -jnp.inf), axis=0, keepdims=True)
+    pl.run_scoped(compute, *[pltpu.ACC(pair % 2)((6 * LEAVES, 2 * HALF), jnp.float32) for pair in range(pairs)])
 
     def report(place):
         step = everyone - place
@@ -213,7 +239,6 @@
     n, n_feat = lax.axis_size("rows"), lax.axis_size("feat")
     rows, local_features = bin_index.shape
     own = local_features // n
-    group = 2 if own % 2 == 0 else 1
     tiles = rows // LANES
     pieces = 4
     everyone = n * n_feat
@@ -221,7 +246,7 @@
     vmem = pl.BlockSpec(memory_space=pltpu.VMEM)
     dma = pltpu.SemaphoreType.DMA
     gain, best = pl.pallas_call(
-        functools.partial(kernel, n, n_feat, group),
+        functools.partial(kernel, n, n_feat),
         out_shape=(pltpu.VMEM((own, LEAVES, BINS), jnp.float32),
                    pltpu.VMEM((1, LEAVES), jnp.float32)),
         in_specs=[pl.BlockSpec(memory_space=pl.ANY)] * 4,
@@ -237,7 +262,6 @@
             pltpu.VMEM((n, own, rows), jnp.bfloat16),
             pltpu.VMEM((n_feat, n, meta_rows, LANES), jnp.bfloat16),
             pltpu.VMEM((2 * LEAVES, rows), jnp.bfloat16),
-            pltpu.VMEM((own, 4 * LEAVES, HALF), jnp.float32),
             pltpu.VMEM((1, LANES), jnp.float32),
             pltpu.VMEM((everyone, 1, LANES), jnp.float32),
             dma((pieces,)), dma((n,)), dma((n,)), dma((n,)), dma((n,)), dma((n_feat,)), dma((n_feat,)), dma((2,)),

time: 29 us -> 28.3 us (0.976)
  Pallas kernels: 27 us -> 26.3 us
    pallas_call x1, Pallas kernels: 27 us -> 26.3 us  [body(): pl.pallas_call(functools.partial(kernel, n, n_feat), out_shape=(pltpu.VME...]
where the time goes in v2:
time: 28.3 us; the launch traced here: 28.2 us
  Pallas kernels  26.3 us (93%)
  local copies, waits for them, and re-layouts  1.22 us (4%)
  between operations  0.64 us (2%)
    pallas_call x1, Pallas kernels, body(): pl.pallas_call(functools.partial(kernel, n, n_feat), out_shape=(pltpu.VME...  26.3 us
    unnamed x2, local copies, waits for them, and re-layouts  1.22 us

profile of v2, /device:TPU:0, one launch (start us, length us, event | category | flops | bytes accessed | tf_op | source)
XLA Modules:
  0.0 28.2 jit_solution(1620961078920622388)
XLA Ops:
  0.6 26.3 %shard_map.59 = (f32[16,16,256]{2,1,0:T(8,128)S(1)}, f32[1,16]{1,0:T(1,128)S(1)}) custom-call(s32[2048,128]{1,0:T(8,128)} %bins_hbm.1, s32[16,128]{1,0:T(8,128)} %bitcast.7, bf16[16,128]{1,0:T(8,128)(2,1)} %bitcast.8, bf16[16,128]{1,0:T(8,128)(2,1)} %bitcast.9), custom_call_target="tpu_custom_call" | custom-call | tf_op jit(solution)/shard_map/pallas_call | solution.py:248
  26.9 0.7 %copy.8 = f32[1,16,16,256]{3,2,1,0:T(8,128)} copy(f32[1,16,16,256]{3,2,1,0:T(8,128)S(1)} %bitcast.5) | data formatting | bytes 524288
  27.7 0.5 %copy.9 = f32[16]{0:T(128)} copy(f32[16]{0:T(128)S(1)} %bitcast.6) | data formatting | bytes 128

commit v3 on v2

--- a/solution.py
+++ b/solution.py
@@ -19,14 +19,15 @@
 
 def kernel(n, n_feat, bins_hbm, leaf_hbm, grad_hbm, hess_hbm, gain_ref, best_ref,
            leaf_ref, grad_ref, hess_ref, small_sems, raw, bins_src, meta_src, columns, metas, weights, top, landing,
-           raw_sems, bin_send, bin_recv, meta_send, meta_recv, swap_send, swap_recv, own_sems, top_send, top_recv):
+           raw_sems, bin_send, bin_recv, near_send, near_recv, far_send, far_recv, swap_send, swap_recv, own_sems,
+           top_send, top_recv):
     me, me_feat = lax.axis_index("rows"), lax.axis_index("feat")
     everyone = n * n_feat
     me_all = me * n_feat + me_feat
     own, rows = bins_src.shape[1], bins_src.shape[2]
     tiles = rows // LANES
     share = tiles // n_feat
-    half = n // 2
+    half, quarter = n // 2, n // 4
     across = (1 - me // half) * half
     pieces = raw_sems.shape[0]
     piece_rows = rows // pieces
@@ -77,7 +78,7 @@
         fetch(piece).wait()
         for tile in range(piece * piece_rows // LANES, (piece + 1) * piece_rows // LANES):
             lanes = slice(tile * LANES, (tile + 1) * LANES)
-            turned = raw[lanes].astype(jnp.float32).T.astype(jnp.bfloat16)
+            turned = raw[lanes].astype(jnp.float32).astype(jnp.bfloat16).T
             bins_src[:, :, lanes] = turned.reshape(n, own, LANES)
 
     own_bins = pltpu.make_async_copy(bins_src.at[me], columns.at[me], own_sems.at[0])
@@ -89,31 +90,59 @@
     def bin_copy(step, landed):
         other = partner(step)
         return pltpu.make_async_remote_copy(
-            src_ref=bins_src.at[other], dst_ref=columns.at[other if landed else me], send_sem=bin_send.at[step],
+            src_ref=bins_src.at[other], dst_ref=columns.at[other if landed else me], send_sem=bin_send,
             recv_sem=bin_recv.at[step], device_id={"rows": other}, device_id_type=MESH)
+
+    def late_copy(step, part, landed):
+        other = partner(step)
+        some = pl.ds(part * (rows // 2), rows // 2)
+        return pltpu.make_async_remote_copy(
+            src_ref=bins_src.at[other, :, some], dst_ref=columns.at[other if landed else me, :, some],
+            send_sem=bin_send, recv_sem=bin_recv.at[step + 2 * part],
+            device_id={"rows": other}, device_id_type=MESH)
+
+    def use_step(place):
+        later = place - 2
+        turns = jnp.where(later % 2 == 0, 2 + later // 2, half + later // 2)
+        near_left = 2 + later - quarter
+        step = jnp.where(later < 2 * quarter, turns, jnp.where(place < half + quarter, near_left, place))
+        return jnp.where(later < 0, place, step)
+
+    def send_step(place):
+        turns = 1 + place // 2 + (place % 2) * (half - 1)
+        return jnp.where(place < half, turns, jnp.where(place < half + quarter - 1, 1 + place - quarter, place + 1))
 
     def near_meta(step, landed):
         other = partner(step)
         return pltpu.make_async_remote_copy(
-            src_ref=meta_src, dst_ref=metas.at[:, other if landed else me], send_sem=meta_send.at[step],
-            recv_sem=meta_recv.at[step], device_id={"rows": other}, device_id_type=MESH)
+            src_ref=meta_src, dst_ref=metas.at[:, other if landed else me], send_sem=near_send,
+            recv_sem=near_recv.at[step], device_id={"rows": other}, device_id_type=MESH)
 
     def far_meta(step, landed):
         other = partner(step)
         return pltpu.make_async_remote_copy(
-            src_ref=meta_src.at[me_feat], dst_ref=metas.at[me_feat, other if landed else me], send_sem=meta_send.at[step],
-            recv_sem=meta_recv.at[step], device_id={"rows": other}, device_id_type=MESH)
+            src_ref=meta_src.at[me_feat], dst_ref=metas.at[me_feat, other if landed else me], send_sem=far_send,
+            recv_sem=far_recv, device_id={"rows": other}, device_id_type=MESH)
+
+    far_rows = metas.at[0, pl.ds(0, half)]
+    near_rows = metas.at[:, pl.ds(0, half - 1)]
+    swapped_rows = metas.at[pl.ds(0, n_feat - 1), pl.ds(0, half)]
+    sent_blocks = columns.at[pl.ds(0, n - 1)]
+    reports = landing.at[pl.ds(1, everyone - 1)]
 
     def swap_meta(step, landed):
         held = lax.rem(me_feat + n_feat - step, n_feat) if landed else me_feat
         far = metas.at[held, pl.ds(across, half)]
         return pltpu.make_async_remote_copy(
-            src_ref=far, dst_ref=far, send_sem=swap_send.at[step], recv_sem=swap_recv.at[step],
+            src_ref=far, dst_ref=far, send_sem=swap_send, recv_sem=swap_recv,
             device_id={"feat": lax.rem(me_feat + step, n_feat)}, device_id_type=MESH)
 
     each(half, n, lambda step: far_meta(step, False).start())
     each(1, half, lambda step: near_meta(step, False).start())
-    each(1, n, lambda step: bin_copy(step, False).start())
+    each(0, n - 3, lambda place: bin_copy(send_step(place), False).start())
+    late = [(step, part) for part in range(2) for step in (n - 2, n - 1)]
+    for step, part in late:
+        late_copy(step, part, False).start()
     landing[0] = jnp.full((1, LANES), -jnp.inf, jnp.float32)
     own_bins.wait()
     own_meta.wait()
@@ -123,7 +152,12 @@
     def compute(*sums):
         for total in sums:
             pltpu.matmul_pop(total)
-        lax.fori_loop(0, n, functools.partial(one_shard, sums), 0)
+        lax.fori_loop(0, n - 2, functools.partial(one_shard, sums), 0)
+        for step, part in late:
+            late_copy(step, part, True).wait_recv()
+            add_rows(sums, partner(step), part * (tiles // 2), (part + 1) * (tiles // 2))
+        for refs, sem in ((sent_blocks, bin_send), (near_rows, near_send), (far_rows, far_send), (swapped_rows, swap_send)):
+            pltpu.make_async_copy(refs, refs, sem).wait()
         largest = jnp.full((LEAVES, HALF), -jnp.inf, jnp.float32)
         for pair in range(pairs):
             largest = gains(pair, pltpu.matmul_pop(sums[pair]), largest)
@@ -132,29 +166,34 @@
                    == lax.broadcasted_iota(jnp.int32, (LEAVES, LANES), 1))
         top[...] = jnp.max(jnp.where(on_lane, largest, -jnp.inf), axis=0, keepdims=True)
 
-    def one_shard(sums, step, carry):
+    def one_shard(sums, place, carry):
+        step = use_step(place)
         origin = partner(step)
 
-        @pl.when(step == min(2, half - 1))
+        @pl.when(place == 2)
         def swap():
-            each(half, n, lambda far: far_meta(far, True).wait_recv())
+            pltpu.make_async_copy(far_rows, far_rows, far_recv).wait()
             each(1, n_feat, lambda other: swap_meta(other, False).start())
 
         @pl.when(jnp.logical_and(step > 0, step < half))
         def near_arrived():
             near_meta(step, True).wait_recv()
 
-        @pl.when(step == half)
+        @pl.when(place == 3)
         def swapped():
-            each(1, n_feat, lambda other: swap_meta(other, True).wait_recv())
+            pltpu.make_async_copy(swapped_rows, swapped_rows, swap_recv).wait()
 
         @pl.when(step > 0)
         def arrived():
             bin_copy(step, True).wait_recv()
 
+        add_rows(sums, origin, 0, tiles)
+        return carry
+
+    def add_rows(sums, origin, first_tile, last_tile):
         table = metas[:, origin].astype(jnp.float32)
         leaf_of = lax.broadcasted_iota(jnp.int32, (LEAVES, LANES), 0).astype(jnp.float32)
-        for tile in range(tiles):
+        for tile in range(first_tile, last_tile):
             piece, row = tile // share, tile % share
             member = jnp.broadcast_to(table[piece, row:row + 1], (LEAVES, LANES)) == leaf_of
             for part in (0, 1):
@@ -163,7 +202,8 @@
                 weights[part * LEAVES:(part + 1) * LEAVES, tile * LANES:(tile + 1) * LANES] = (
                     jnp.where(member, value, 0.0).astype(jnp.bfloat16))
 
-        block = columns[origin]
+        begin = first_tile * LANES
+        block = columns[origin, :, begin:last_tile * LANES]
         low = jnp.where(block >= HALF, block - HALF, block)
         level = lax.broadcasted_iota(jnp.int32, (HALF, DEPTH), 0).astype(jnp.bfloat16)
         zero = jnp.zeros((), jnp.bfloat16)
@@ -178,9 +218,9 @@
             return jnp.where(upper, table_rows, zero)
 
         for first in range(0, pairs, 2):
-            for chunk in range(rows // DEPTH):
+            for chunk in range(block.shape[1] // DEPTH):
                 lanes = slice(chunk * DEPTH, (chunk + 1) * DEPTH)
-                table_rows = weights[:, lanes]
+                table_rows = weights[:, begin + chunk * DEPTH:begin + (chunk + 1) * DEPTH]
                 for pair in range(first, min(first + 2, pairs)):
                     features = (2 * pair, min(2 * pair + 1, own - 1))
                     steps = jnp.concatenate([step_of(feature, lanes) for feature in features], axis=0)
@@ -192,7 +232,6 @@
                         sums[pair],
                         jnp.concatenate([table_rows] + [upper_of(feature, lanes, table_rows) for feature in features], axis=0),
                         load_staged_rhs=chunk % 2)
-        return carry
 
     def gains(pair, part, largest):
         for place in range(2):
@@ -202,14 +241,13 @@
             lanes = slice(place * HALF, (place + 1) * HALF)
             both = part[:2 * LEAVES, lanes]
             upper = part[(1 + place) * 2 * LEAVES:(2 + place) * 2 * LEAVES, lanes]
-            lower = both - upper
-            grad_low, hess_low = lower[:LEAVES], lower[LEAVES:]
-            grad_high = upper[:LEAVES] + grad_low[:, HALF - 1:]
-            hess_high = upper[LEAVES:] + hess_low[:, HALF - 1:]
-            total_grad, total_hess = grad_high[:, HALF - 1:], hess_high[:, HALF - 1:]
+            total = both[:, HALF - 1:]
+            lower, beyond = both - upper, upper[:, HALF - 1:] - upper
+            total_grad, total_hess = total[:LEAVES], total[LEAVES:]
             whole = total_grad * total_grad / (total_hess + reg_lambda)
-            for side, left_grad, left_hess in ((0, grad_low, hess_low), (1, grad_high, hess_high)):
-                right_grad, right_hess = total_grad - left_grad, total_hess - left_hess
+            for side, left, right in ((0, lower, total - lower), (1, total - beyond, beyond)):
+                left_grad, left_hess = left[:LEAVES], left[LEAVES:]
+                right_grad, right_hess = right[:LEAVES], right[LEAVES:]
                 gain = 0.5 * (left_grad * left_grad / (left_hess + reg_lambda)
                               + right_grad * right_grad / (right_hess + reg_lambda) - whole)
                 gain_ref[feature, :, side * HALF:(side + 1) * HALF] = gain
@@ -221,17 +259,13 @@
     def report(place):
         step = everyone - place
         return pltpu.make_async_remote_copy(
-            src_ref=top, dst_ref=landing.at[step], send_sem=top_send.at[step],
-            recv_sem=top_recv.at[step], device_id=device_after(step), device_id_type=MESH)
+            src_ref=top, dst_ref=landing.at[step], send_sem=top_send,
+            recv_sem=top_recv, device_id=device_after(step), device_id_type=MESH)
 
     each(1, everyone, lambda place: report(place).start())
-    each(1, n, lambda step: bin_copy(step, False).wait_send())
-    each(1, half, lambda step: near_meta(step, False).wait_send())
-    each(half, n, lambda step: far_meta(step, False).wait_send())
-    each(1, n_feat, lambda step: swap_meta(step, False).wait_send())
-    each(1, everyone, lambda place: report(everyone - place).wait_recv())
+    pltpu.make_async_copy(reports, reports, top_recv).wait()
     best = jnp.maximum(top[...], jnp.max(landing[...], axis=0))
-    each(1, everyone, lambda step: report(step).wait_send())
+    pltpu.make_async_copy(reports, reports, top_send).wait()
     best_ref[...] = best[:, :LEAVES]
 
 
@@ -240,8 +274,9 @@
     rows, local_features = bin_index.shape
     own = local_features // n
     tiles = rows // LANES
-    pieces = 4
+    pieces = 1
     everyone = n * n_feat
+    half = n // 2
     meta_rows = -(-3 * (tiles // n_feat) // 16) * 16
     vmem = pl.BlockSpec(memory_space=pltpu.VMEM)
     dma = pltpu.SemaphoreType.DMA
@@ -264,8 +299,7 @@
             pltpu.VMEM((2 * LEAVES, rows), jnp.bfloat16),
             pltpu.VMEM((1, LANES), jnp.float32),
             pltpu.VMEM((everyone, 1, LANES), jnp.float32),
-            dma((pieces,)), dma((n,)), dma((n,)), dma((n,)), dma((n,)), dma((n_feat,)), dma((n_feat,)), dma((2,)),
-            dma((everyone,)), dma((everyone,)),
+            dma((pieces,)), dma, dma((n + 2,)), dma, dma((half,)), dma, dma, dma, dma, dma((2,)), dma, dma,
         ],
         compiler_params=pltpu.CompilerParams(
             collective_id=0, has_side_effects=True, vmem_limit_bytes=60 * 1024 * 1024),

time: 28.3 us -> 27.5 us (0.972)
  Pallas kernels: 26.3 us -> 25.4 us
    pallas_call x1, Pallas kernels: 26.3 us -> 25.4 us  [body(): pl.pallas_call(functools.partial(kernel, n, n_feat), out_shape=(pltpu.VME...]
where the time goes in v3:
time: 27.5 us; the launch traced here: 27.3 us
  Pallas kernels  25.4 us (92%)
  local copies, waits for them, and re-layouts  1.22 us (4%)
  between operations  0.64 us (2%)
    pallas_call x1, Pallas kernels, body(): pl.pallas_call(functools.partial(kernel, n, n_feat), out_shape=(pltpu.VME...  25.4 us
    unnamed x2, local copies, waits for them, and re-layouts  1.22 us

profile of v3, /device:TPU:0, one launch (start us, length us, event | category | flops | bytes accessed | tf_op | source)
XLA Modules:
  0.0 27.3 jit_solution(6376857560769152233)
XLA Ops:
  0.6 25.4 %shard_map.59 = (f32[16,16,256]{2,1,0:T(8,128)S(1)}, f32[1,16]{1,0:T(1,128)S(1)}) custom-call(s32[2048,128]{1,0:T(8,128)} %bins_hbm.1, s32[16,128]{1,0:T(8,128)} %bitcast.7, bf16[16,128]{1,0:T(8,128)(2,1)} %bitcast.8, bf16[16,128]{1,0:T(8,128)(2,1)} %bitcast.9), custom_call_target="tpu_custom_call" | custom-call | tf_op jit(solution)/shard_map/pallas_call | solution.py:283
  26.0 0.7 %copy.8 = f32[1,16,16,256]{3,2,1,0:T(8,128)} copy(f32[1,16,16,256]{3,2,1,0:T(8,128)S(1)} %bitcast.5) | data formatting | bytes 524288
  26.8 0.5 %copy.9 = f32[16]{0:T(128)} copy(f32[16]{0:T(128)S(1)} %bitcast.6) | data formatting | bytes 128

commit v4 on v3

--- a/solution.py
+++ b/solution.py
@@ -20,7 +20,7 @@
 def kernel(n, n_feat, bins_hbm, leaf_hbm, grad_hbm, hess_hbm, gain_ref, best_ref,
            leaf_ref, grad_ref, hess_ref, small_sems, raw, bins_src, meta_src, columns, metas, weights, top, landing,
            raw_sems, bin_send, bin_recv, near_send, near_recv, far_send, far_recv, swap_send, swap_recv, own_sems,
-           top_send, top_recv):
+           top_send, top_recv, side_in, tally):
     me, me_feat = lax.axis_index("rows"), lax.axis_index("feat")
     everyone = n * n_feat
     me_all = me * n_feat + me_feat
@@ -28,12 +28,12 @@
     tiles = rows // LANES
     share = tiles // n_feat
     half, quarter = n // 2, n // 4
-    across = (1 - me // half) * half
+    side, across = me % 2, (1 - me // half) * quarter
     pieces = raw_sems.shape[0]
     piece_rows = rows // pieces
 
-    def fetch(piece):
-        span = pl.ds(piece * piece_rows, piece_rows)
+    def fetch(piece, first=0, count=piece_rows):
+        span = pl.ds(piece * piece_rows + first, count)
         return pltpu.make_async_copy(bins_hbm.at[span], raw.at[span], raw_sems.at[piece])
 
     small = [pltpu.make_async_copy(source, target, small_sems.at[place]) for place, (source, target) in enumerate(
@@ -41,7 +41,8 @@
     for copy in small:
         copy.start()
     for piece in range(pieces):
-        fetch(piece).start()
+        for first in range(0, piece_rows, 2 * LANES):
+            fetch(piece, first, 2 * LANES).start()
 
     def partner(step):
         other, bit = 0, 1
@@ -64,7 +65,8 @@
     def greet(device):
         pl.semaphore_signal(barrier, inc=1, device_id=device, device_id_type=MESH)
 
-    each(1, n, lambda step: greet({"rows": partner(n - step)}))
+    each(1, half, lambda turn: greet({"rows": partner(n - 2 * turn)}))
+    greet({"rows": partner(1)})
     each(1, n_feat, lambda step: greet(device_after(step)))
 
     for copy in small:
@@ -82,10 +84,10 @@
             bins_src[:, :, lanes] = turned.reshape(n, own, LANES)
 
     own_bins = pltpu.make_async_copy(bins_src.at[me], columns.at[me], own_sems.at[0])
-    own_meta = pltpu.make_async_copy(meta_src, metas.at[:, me], own_sems.at[1])
+    own_meta = pltpu.make_async_copy(meta_src, metas.at[:, me % 2, me // 2], own_sems.at[1])
     own_bins.start()
     own_meta.start()
-    pl.semaphore_wait(barrier, n - 1 + n_feat - 1)
+    pl.semaphore_wait(barrier, half + n_feat - 1)
 
     def bin_copy(step, landed):
         other = partner(step)
@@ -114,35 +116,45 @@
 
     def near_meta(step, landed):
         other = partner(step)
-        return pltpu.make_async_remote_copy(
-            src_ref=meta_src, dst_ref=metas.at[:, other if landed else me], send_sem=near_send,
+        row = other if landed else me
+        return pltpu.make_async_remote_copy(
+            src_ref=meta_src, dst_ref=metas.at[:, row % 2, row // 2], send_sem=near_send,
             recv_sem=near_recv.at[step], device_id={"rows": other}, device_id_type=MESH)
 
-    def far_meta(step, landed):
-        other = partner(step)
-        return pltpu.make_async_remote_copy(
-            src_ref=meta_src.at[me_feat], dst_ref=metas.at[me_feat, other if landed else me], send_sem=far_send,
-            recv_sem=far_recv, device_id={"rows": other}, device_id_type=MESH)
-
-    far_rows = metas.at[0, pl.ds(0, half)]
-    near_rows = metas.at[:, pl.ds(0, half - 1)]
-    swapped_rows = metas.at[pl.ds(0, n_feat - 1), pl.ds(0, half)]
+    def far_meta(step):
+        return pltpu.make_async_remote_copy(
+            src_ref=meta_src.at[me_feat], dst_ref=metas.at[me_feat, side, me // 2], send_sem=far_send,
+            recv_sem=far_recv, device_id={"rows": partner(step)}, device_id_type=MESH)
+
+    far_rows = metas.at[0, 0, pl.ds(0, quarter)]
+    near_rows = metas.at[:, 0, pl.ds(0, half - 1)]
     sent_blocks = columns.at[pl.ds(0, n - 1)]
     reports = landing.at[pl.ds(1, everyone - 1)]
 
-    def swap_meta(step, landed):
-        held = lax.rem(me_feat + n_feat - step, n_feat) if landed else me_feat
-        far = metas.at[held, pl.ds(across, half)]
+    def swap_meta(step):
+        far = metas.at[me_feat, side, pl.ds(across, quarter)]
         return pltpu.make_async_remote_copy(
             src_ref=far, dst_ref=far, send_sem=swap_send, recv_sem=swap_recv,
-            device_id={"feat": lax.rem(me_feat + step, n_feat)}, device_id_type=MESH)
-
-    each(half, n, lambda step: far_meta(step, False).start())
-    each(1, half, lambda step: near_meta(step, False).start())
-    each(0, n - 3, lambda place: bin_copy(send_step(place), False).start())
+            device_id={"rows": partner(1) if step >= n_feat else me, "feat": lax.rem(me_feat + step % n_feat, n_feat)},
+            device_id_type=MESH)
+
+    def await_swaps(sem):
+        pltpu.make_async_copy(tally, tally, sem).wait()
+
+    pl.semaphore_signal(side_in, inc=1, device_id={"rows": partner(1)}, device_id_type=MESH)
+    each(quarter, half, lambda turn: far_meta(2 * turn).start())
+    near_meta(1, False).start()
+    each(1, quarter, lambda turn: near_meta(2 * turn, False).start())
     late = [(step, part) for part in range(2) for step in (n - 2, n - 1)]
-    for step, part in late:
-        late_copy(step, part, False).start()
+    each(0, 2, lambda place: bin_copy(send_step(place), False).start())
+
+    def send_rest():
+        pl.semaphore_wait(side_in, 1)
+        each(1, quarter, lambda turn: near_meta(2 * turn + 1, False).start())
+        each(2, n - 3, lambda place: bin_copy(send_step(place), False).start())
+        for step, part in late:
+            late_copy(step, part, False).start()
+
     landing[0] = jnp.full((1, LANES), -jnp.inf, jnp.float32)
     own_bins.wait()
     own_meta.wait()
@@ -153,11 +165,12 @@
         for total in sums:
             pltpu.matmul_pop(total)
         lax.fori_loop(0, n - 2, functools.partial(one_shard, sums), 0)
-        for step, part in late:
+        for step, part in sorted(late):
             late_copy(step, part, True).wait_recv()
             add_rows(sums, partner(step), part * (tiles // 2), (part + 1) * (tiles // 2))
-        for refs, sem in ((sent_blocks, bin_send), (near_rows, near_send), (far_rows, far_send), (swapped_rows, swap_send)):
+        for refs, sem in ((sent_blocks, bin_send), (near_rows, near_send), (far_rows, far_send)):
             pltpu.make_async_copy(refs, refs, sem).wait()
+        await_swaps(swap_send)
         largest = jnp.full((LEAVES, HALF), -jnp.inf, jnp.float32)
         for pair in range(pairs):
             largest = gains(pair, pltpu.matmul_pop(sums[pair]), largest)
@@ -170,10 +183,13 @@
         step = use_step(place)
         origin = partner(step)
 
+        pl.when(place == 1)(send_rest)
+
         @pl.when(place == 2)
         def swap():
             pltpu.make_async_copy(far_rows, far_rows, far_recv).wait()
-            each(1, n_feat, lambda other: swap_meta(other, False).start())
+            for other in range(1, 2 * n_feat):
+                swap_meta(other).start()
 
         @pl.when(jnp.logical_and(step > 0, step < half))
         def near_arrived():
@@ -181,7 +197,7 @@
 
         @pl.when(place == 3)
         def swapped():
-            pltpu.make_async_copy(swapped_rows, swapped_rows, swap_recv).wait()
+            await_swaps(swap_recv)
 
         @pl.when(step > 0)
         def arrived():
@@ -191,7 +207,7 @@
         return carry
 
     def add_rows(sums, origin, first_tile, last_tile):
-        table = metas[:, origin].astype(jnp.float32)
+        table = metas[:, origin % 2, origin // 2].astype(jnp.float32)
         leaf_of = lax.broadcasted_iota(jnp.int32, (LEAVES, LANES), 0).astype(jnp.float32)
         for tile in range(first_tile, last_tile):
             piece, row = tile // share, tile % share
@@ -274,7 +290,7 @@
     rows, local_features = bin_index.shape
     own = local_features // n
     tiles = rows // LANES
-    pieces = 1
+    pieces = 2
     everyone = n * n_feat
     half = n // 2
     meta_rows = -(-3 * (tiles // n_feat) // 16) * 16
@@ -295,11 +311,12 @@
             pltpu.VMEM((n, own, rows), jnp.bfloat16),
             pltpu.VMEM((n_feat, meta_rows, LANES), jnp.bfloat16),
             pltpu.VMEM((n, own, rows), jnp.bfloat16),
-            pltpu.VMEM((n_feat, n, meta_rows, LANES), jnp.bfloat16),
+            pltpu.VMEM((n_feat, 2, half, meta_rows, LANES), jnp.bfloat16),
             pltpu.VMEM((2 * LEAVES, rows), jnp.bfloat16),
             pltpu.VMEM((1, LANES), jnp.float32),
             pltpu.VMEM((everyone, 1, LANES), jnp.float32),
-            dma((pieces,)), dma, dma((n + 2,)), dma, dma((half,)), dma, dma, dma, dma, dma((2,)), dma, dma,
+            dma((pieces,)), dma, dma((n + 2,)), dma, dma((half,)), dma, dma, dma, dma, dma((2,)), dma, dma, pltpu.SemaphoreType.REGULAR,
+            pltpu.VMEM((2 * n_feat - 1, n // 4, meta_rows, LANES), jnp.bfloat16),
         ],
         compiler_params=pltpu.CompilerParams(
             collective_id=0, has_side_effects=True, vmem_limit_bytes=60 * 1024 * 1024),

time: 27.5 us -> 26.7 us (0.971)
  Pallas kernels: 25.4 us -> 24.7 us
    pallas_call x1, Pallas kernels: 25.4 us -> 24.7 us  [body(): pl.pallas_call(functools.partial(kernel, n, n_feat), out_shape=(pltpu.VME...]
where the time goes in v4:
time: 26.7 us; the launch traced here: 26.6 us
  Pallas kernels  24.7 us (93%)
  local copies, waits for them, and re-layouts  1.22 us (5%)
  between operations  0.64 us (2%)
    pallas_call x1, Pallas kernels, body(): pl.pallas_call(functools.partial(kernel, n, n_feat), out_shape=(pltpu.VME...  24.7 us
    unnamed x2, local copies, waits for them, and re-layouts  1.22 us

profile of v4, /device:TPU:0, one launch (start us, length us, event | category | flops | bytes accessed | tf_op | source)
XLA Modules:
  0.0 26.6 jit_solution(138028897880858014)
XLA Ops:
  0.6 24.7 %shard_map.59 = (f32[16,16,256]{2,1,0:T(8,128)S(1)}, f32[1,16]{1,0:T(1,128)S(1)}) custom-call(s32[2048,128]{1,0:T(8,128)} %bins_hbm.1, s32[16,128]{1,0:T(8,128)} %bitcast.7, bf16[16,128]{1,0:T(8,128)(2,1)} %bitcast.8, bf16[16,128]{1,0:T(8,128)(2,1)} %bitcast.9), custom_call_target="tpu_custom_call" | custom-call | tf_op jit(solution)/shard_map/pallas_call | solution.py:299
  25.4 0.7 %copy.8 = f32[1,16,16,256]{3,2,1,0:T(8,128)} copy(f32[1,16,16,256]{3,2,1,0:T(8,128)S(1)} %bitcast.5) | data formatting | bytes 524288
  26.1 0.5 %copy.9 = f32[16]{0:T(128)} copy(f32[16]{0:T(128)S(1)} %bitcast.6) | data formatting | bytes 128

commit v5 on v4

--- a/solution.py
+++ b/solution.py
@@ -152,7 +152,7 @@
         pl.semaphore_wait(side_in, 1)
         each(1, quarter, lambda turn: near_meta(2 * turn + 1, False).start())
         each(2, n - 3, lambda place: bin_copy(send_step(place), False).start())
-        for step, part in late:
+        for step, part in sorted(late):
             late_copy(step, part, False).start()
 
     landing[0] = jnp.full((1, LANES), -jnp.inf, jnp.float32)
@@ -164,6 +164,7 @@
     def compute(*sums):
         for total in sums:
             pltpu.matmul_pop(total)
+        send_rest()
         lax.fori_loop(0, n - 2, functools.partial(one_shard, sums), 0)
         for step, part in sorted(late):
             late_copy(step, part, True).wait_recv()
@@ -182,8 +183,6 @@
     def one_shard(sums, place, carry):
         step = use_step(place)
         origin = partner(step)
-
-        pl.when(place == 1)(send_rest)
 
         @pl.when(place == 2)
         def swap():

time: 26.7 us -> 26.4 us (0.989)
  Pallas kernels: 24.7 us -> 24.4 us
    pallas_call x1, Pallas kernels: 24.7 us -> 24.4 us  [body(): pl.pallas_call(functools.partial(kernel, n, n_feat), out_shape=(pltpu.VME...]
where the time goes in v5:
time: 26.4 us; the launch traced here: 26.3 us
  Pallas kernels  24.4 us (92%)
  local copies, waits for them, and re-layouts  1.22 us (5%)
  between operations  0.64 us (2%)
    pallas_call x1, Pallas kernels, body(): pl.pallas_call(functools.partial(kernel, n, n_feat), out_shape=(pltpu.VME...  24.4 us
    unnamed x2, local copies, waits for them, and re-layouts  1.22 us

profile of v5, /device:TPU:0, one launch (start us, length us, event | category | flops | bytes accessed | tf_op | source)
XLA Modules:
  0.0 26.3 jit_solution(10983017966629471880)
XLA Ops:
  0.6 24.4 %shard_map.59 = (f32[16,16,256]{2,1,0:T(8,128)S(1)}, f32[1,16]{1,0:T(1,128)S(1)}) custom-call(s32[2048,128]{1,0:T(8,128)} %bins_hbm.1, s32[16,128]{1,0:T(8,128)} %bitcast.7, bf16[16,128]{1,0:T(8,128)(2,1)} %bitcast.8, bf16[16,128]{1,0:T(8,128)(2,1)} %bitcast.9), custom_call_target="tpu_custom_call" | custom-call | tf_op jit(solution)/shard_map/pallas_call | solution.py:298
  25.1 0.7 %copy.8 = f32[1,16,16,256]{3,2,1,0:T(8,128)} copy(f32[1,16,16,256]{3,2,1,0:T(8,128)S(1)} %bitcast.5) | data formatting | bytes 524288
  25.8 0.5 %copy.9 = f32[16]{0:T(128)} copy(f32[16]{0:T(128)S(1)} %bitcast.6) | data formatting | bytes 128

commit v6 on v5

--- a/solution.py
+++ b/solution.py
@@ -146,12 +146,12 @@
     near_meta(1, False).start()
     each(1, quarter, lambda turn: near_meta(2 * turn, False).start())
     late = [(step, part) for part in range(2) for step in (n - 2, n - 1)]
-    each(0, 2, lambda place: bin_copy(send_step(place), False).start())
+    each(0, 3, lambda place: bin_copy(send_step(place), False).start())
 
     def send_rest():
         pl.semaphore_wait(side_in, 1)
         each(1, quarter, lambda turn: near_meta(2 * turn + 1, False).start())
-        each(2, n - 3, lambda place: bin_copy(send_step(place), False).start())
+        each(3, n - 3, lambda place: bin_copy(send_step(place), False).start())
         for step, part in sorted(late):
             late_copy(step, part, False).start()
 

time: 26.4 us -> 26.4 us (level)
  no operation moved by 1% of the time
where the time goes in v6:
time: 26.4 us; the launch traced here: 26.2 us
  Pallas kernels  24.4 us (92%)
  local copies, waits for them, and re-layouts  1.22 us (5%)
  between operations  0.64 us (2%)
    pallas_call x1, Pallas kernels, body(): pl.pallas_call(functools.partial(kernel, n, n_feat), out_shape=(pltpu.VME...  24.4 us
    unnamed x2, local copies, waits for them, and re-layouts  1.22 us

profile of v6, /device:TPU:0, one launch (start us, length us, event | category | flops | bytes accessed | tf_op | source)
XLA Modules:
  0.0 26.2 jit_solution(3406756963650327208)
XLA Ops:
  0.6 24.4 %shard_map.59 = (f32[16,16,256]{2,1,0:T(8,128)S(1)}, f32[1,16]{1,0:T(1,128)S(1)}) custom-call(s32[2048,128]{1,0:T(8,128)} %bins_hbm.1, s32[16,128]{1,0:T(8,128)} %bitcast.7, bf16[16,128]{1,0:T(8,128)(2,1)} %bitcast.8, bf16[16,128]{1,0:T(8,128)(2,1)} %bitcast.9), custom_call_target="tpu_custom_call" | custom-call | tf_op jit(solution)/shard_map/pallas_call | solution.py:298
  25.0 0.7 %copy.8 = f32[1,16,16,256]{3,2,1,0:T(8,128)} copy(f32[1,16,16,256]{3,2,1,0:T(8,128)S(1)} %bitcast.5) | data formatting | bytes 524288
  25.7 0.5 %copy.9 = f32[16]{0:T(128)} copy(f32[16]{0:T(128)S(1)} %bitcast.6) | data formatting | bytes 128
